TPU v7x, 32 devices: a whole 2x2x4 slice. The times are simulated.
32 devices in a mesh: rows: 8 (over z, y), sub: 4 (over x, core).
Axes of the slice: x: 2, y: 2, z: 4, core: 2. Of those that a mesh axis runs over, the one named last changes fastest.
Arguments:
- frames: float32 [15, 32768], P(None, ('rows', 'sub')), may hold values from -1 to 1, as said below
- start_vector: float32 [3, 32768], P(None, ('rows', 'sub')), may hold values from -12 to 12
- edge_blocks: float32 [36, 65536], P(None, ('rows', 'sub')), may hold values from -14.4 to 14.4
- edge_source: int32 [32, 2048], P(('rows', 'sub')), may hold values from 0 to 1023
- edge_target: int32 [32, 2048], P(('rows', 'sub')), may hold values from 0 to 1535, as said below
- edge_count: int32 [32], P(('rows', 'sub')), may hold values from 1024 to 2048, as said below
- send_index: int32 [32, 512], P(('rows', 'sub')), may hold values from 0 to 1024, as said below
Outputs:
- new_frames: float32 [15, 32768], P(None, ('rows', 'sub'))
- last_vector: float32 [3, 32768], P(None, ('rows', 'sub'))
- tridiagonal: float32 [2, 4], replicated
Inputs may be any that keep to these rules, and one draw needn't show every extreme that they name: `frames`: each pose's block has orthonormal columns to float32 rounding. `edge_target`: below 1024: a pose of the same device. 1024 + u: halo slot u, whose block u // 16 on the providing device is never empty. `edge_count`: some device uses all 2048 slots. `send_index`: row q holds, in blocks of 16, the local poses that device q provides to device p (block p); a block is all poses or all 1024, which marks it empty; a device's block for itself is empty.
All inputs are finite; a program needn't handle non-finite values.
Results may differ from a plain program's by a relative error of at most 0.0003.
Values sent between devices are 32-bit elements; how exact they have to be, the bound alone decides.
A program may use at most 64 MiB of HBM per device.

v0:
```python
import jax
import jax.numpy as jnp
from jax import lax
from jax.sharding import PartitionSpec as P

RANK = 5
DIM = 3
LANCZOS = 4
polar_steps = 8
step_length = 0.3
epsilon = 1e-06


def symmetric(edge_blocks):
    blocks_six = edge_blocks.reshape(6, 6, -1)
    return 0.5 * (blocks_six + blocks_six.transpose(1, 0, 2))


def block_product(matrix, field_in):
    return jnp.sum(matrix[None, :, :, :] * field_in[:, None, :, :], axis=2)


def multiplier(left_field, right_field):
    product = jnp.sum(left_field[:, :, None, :] * right_field[:, None, :, :], axis=0)
    return 0.5 * (product + product.transpose(1, 0, 2))


def right_product(field_in, matrix):
    return jnp.sum(field_in[:, :, None, :] * matrix[None, :, :, :], axis=1)


def take_columns(table, index):
    return jnp.take(table, index, axis=1, mode="fill", fill_value=0.0)


def add_columns(values, index, width):
    total = jnp.zeros((values.shape[0], width), jnp.float32)
    return total.at[:, index].add(values, mode="drop")


def pack_rows(field_in, send_row):
    flattened = field_in.reshape(-1, field_in.shape[-1])
    return take_columns(flattened, send_row)


def return_rows(returned, send_row, poses_here):
    return add_columns(returned, send_row, poses_here)


def edge_terms(field_in, halo_vals, coupling, source, target, weight):
    copies = field_in.shape[0]
    poses_here = field_in.shape[2]
    edge_total = source.shape[0]
    extended = jnp.concatenate([field_in, halo_vals.reshape(copies, DIM, -1)], axis=2)
    full_width = extended.shape[2]
    values_first = take_columns(field_in.reshape(copies * DIM, poses_here), source).reshape(
        copies, DIM, edge_total
    )
    values_second = take_columns(extended.reshape(copies * DIM, full_width), target).reshape(
        copies, DIM, edge_total
    )
    upper_part = block_product(coupling[:3, :3], values_first) + block_product(
        coupling[:3, 3:], values_second
    )
    lower_part = block_product(coupling[3:, :3], values_first) + block_product(
        coupling[3:, 3:], values_second
    )
    upper_sum = add_columns(
        (upper_part * weight).reshape(copies * DIM, edge_total), source, poses_here
    )
    lower_sum = add_columns(
        (lower_part * weight).reshape(copies * DIM, edge_total), target, full_width
    )
    home_part = (upper_sum + lower_sum[:, :poses_here]).reshape(copies, DIM, poses_here)
    far_part = lower_sum[:, poses_here:].reshape(copies, DIM, full_width - poses_here)
    return (home_part, far_part)


def retract(frame_now, gradient, length):
    moved = frame_now - length * gradient
    norms = jnp.sum(moved * moved, axis=(0, 1))
    polar_now = moved * jnp.sqrt(DIM / norms)[None, None, :]
    identity = jnp.eye(DIM, dtype=jnp.float32)[:, :, None]
    for iteration in range(polar_steps):
        gram_matrix = jnp.sum(polar_now[:, :, None, :] * polar_now[:, None, :, :], axis=0)
        polar_now = right_product(polar_now, 1.5 * identity - 0.5 * gram_matrix)
    return polar_now


def on_device(frames, start_vector, edge_blocks, edge_source, edge_target, edge_count, send_index):
    poses_here = frames.shape[1]
    shards = lax.axis_size("rows") * lax.axis_size("sub")
    coupling = symmetric(edge_blocks)
    source = edge_source[0]
    target = edge_target[0]
    send_row = send_index[0]
    weight = (jnp.arange(source.shape[0], dtype=jnp.int32) < edge_count[0]).astype(jnp.float32)

    def split_product(field_in, halo_vals):
        return edge_terms(field_in, halo_vals, coupling, source, target, weight)

    frame_now = frames.reshape(RANK, DIM, poses_here)
    halo_vals = lax.all_to_all(
        pack_rows(frame_now, send_row), ("rows", "sub"), split_axis=1, concat_axis=1, tiled=True
    )
    near_part, far_part = split_product(frame_now, halo_vals)
    returned = lax.all_to_all(
        far_part.reshape(RANK * DIM, -1), ("rows", "sub"), split_axis=1, concat_axis=1, tiled=True
    )
    euclidean = near_part + return_rows(returned, send_row, poses_here).reshape(
        RANK, DIM, poses_here
    )
    multipliers = multiplier(frame_now, euclidean)
    gradient = 2.0 * (euclidean - right_product(frame_now, multipliers))
    total_square = lax.psum(jnp.sum(gradient * gradient), ("rows", "sub"))
    length = (
        step_length * jnp.sqrt(jnp.float32(poses_here * shards)) / jnp.sqrt(total_square + epsilon)
    )
    retracted = retract(frame_now, gradient, length)
    halo_moved = lax.all_to_all(
        pack_rows(retracted, send_row), ("rows", "sub"), split_axis=1, concat_axis=1, tiled=True
    )
    near_moved, far_moved = split_product(retracted, halo_moved)
    returned_moved = lax.all_to_all(
        far_moved.reshape(RANK * DIM, -1), ("rows", "sub"), split_axis=1, concat_axis=1, tiled=True
    )
    product_new = near_moved + return_rows(returned_moved, send_row, poses_here).reshape(
        RANK, DIM, poses_here
    )
    certificate_mult = multiplier(retracted, product_new)
    entries = DIM * poses_here * shards
    start_square = lax.psum(jnp.sum(start_vector * start_vector), ("rows", "sub"))
    start_field = start_vector.reshape(1, DIM, poses_here)
    krylov_basis = [start_field / jnp.sqrt(start_square / entries + epsilon)]
    alpha_list = []
    beta_list = []
    for iteration in range(LANCZOS):
        vector = krylov_basis[-1]
        halo_vector = lax.all_to_all(
            pack_rows(vector, send_row), ("rows", "sub"), split_axis=1, concat_axis=1, tiled=True
        )
        near_vector, far_vector = split_product(vector, halo_vector)
        returned_vector = lax.all_to_all(
            far_vector.reshape(DIM, -1), ("rows", "sub"), split_axis=1, concat_axis=1, tiled=True
        )
        image_vec = near_vector + return_rows(returned_vector, send_row, poses_here).reshape(
            1, DIM, poses_here
        )
        image_vec = image_vec - right_product(vector, certificate_mult)
        local_dots = jnp.stack([jnp.sum(member * image_vec) for member in krylov_basis])
        summed_dots, square_total = lax.psum(
            (local_dots, jnp.sum(image_vec * image_vec)), ("rows", "sub")
        )
        projected = summed_dots / entries
        for position in range(len(krylov_basis)):
            image_vec = image_vec - projected[position] * krylov_basis[position]
        beta_now = jnp.sqrt(square_total / entries - jnp.sum(projected * projected) + epsilon)
        krylov_basis.append(image_vec / beta_now)
        alpha_list.append(projected[-1])
        beta_list.append(beta_now)
    tridiagonal = jnp.stack([jnp.stack(alpha_list), jnp.stack(beta_list)])
    return (
        retracted.reshape(RANK * DIM, poses_here),
        krylov_basis[-1].reshape(DIM, poses_here),
        tridiagonal,
    )


def solution(mesh):
    in_specs = (
        P(None, ("rows", "sub")),
        P(None, ("rows", "sub")),
        P(None, ("rows", "sub")),
        P(("rows", "sub"), None),
        P(("rows", "sub"), None),
        P(("rows", "sub")),
        P(("rows", "sub"), None),
    )
    out_specs = (P(None, ("rows", "sub")), P(None, ("rows", "sub")), P())
    return jax.shard_map(
        on_device, mesh=mesh, in_specs=in_specs, out_specs=out_specs, check_vma=False
    )
```

profile of v0, /device:TPU:0, one launch (start us, length us, event | category | flops | bytes accessed | tf_op | source)
XLA Modules:
  0.0 608.0 jit_solution(1578713201348669233)
XLA Ops:
  4.7 7.3 %all-to-all-start = ((f32[32,1,240]{2,1,0:T(1,128)}), f32[32,1,240]{2,1,0:T(1,128)S(1)}, u32[]{:S(2)}, u32[]{:S(2)}) async-start(f32[32,1,240]{2,1,0:T(1,128)} %reshape.1031), calls=%async_computation | async-start | bytes 65536 | tf_op jit(solution)/shard_map/all_to_all | solution.py:103
  14.0 5.5 gather_fusion
  24.2 5.5 gather_fusion.2
  31.8 11.7 %scatter_custom_fusion = f32[15,1536]{0,1:T(8,128)S(1)} fusion(s32[2048]{0:T(1024)S(1)} %bitcast.201, f32[2048,15]{1,0:T(8,128)S(1)} %copy.377, f32[]{:T(128)} %constant.61.clone.1), kind=kCustom, calls=%fused_computation.68 | custom fusion | flops 30720 | bytes 92164 | tf_op jit(solution)/shard_map/scatter-add | solution.py:38
  44.3 5.8 all-to-all-start.1
  51.2 11.7 %scatter_fusion = f32[15,1024]{0,1:T(8,128)S(1)} fusion(f32[15,1024]{0,1:T(8,128)S(1)} %slice-done.1, s32[2048]{0:T(1024)S(1)} %bitcast.183, f32[2048,15]{1,0:T(8,128)S(1)} %copy.378), kind=kCustom, calls=%fused_computation.19 | custom fusion | flops 30720 | bytes 376832 | tf_op jit(solution)/shard_map/scatter-add | solution.py:38
  64.0 2.6 scatter_custom_fusion.2
  67.7 40.7 %all-reduce.4 = (f32[]{:T(128)}, f32[]{:T(128)}) all-reduce(f32[]{:T(128)} %get-tuple-element.95, f32[]{:T(128)} %multiply_reduce_fusion.63), channel_id=1, replica_groups=mesh['rows'=8,'sub'=4] {'rows','sub'}, use_global_device_ids=true, to_apply=%region_10.14 | all-reduce | flops 2 | bytes 16 | tf_op jit(solution)/shard_map/psum | solution.py:115
  113.8 5.5 gather_fusion.6
  122.4 5.5 gather_fusion.3
  130.0 4.9 all-to-all-start.2
  138.5 3.7 all-to-all-done.2
  142.2 2.6 all-to-all-start.4
  146.5 5.5 gather_fusion.5
  154.3 11.8 %scatter_custom_fusion.3 = f32[3,1536]{0,1:T(8,128)S(1)} fusion(s32[2048]{0:T(1024)} %bitcast.202, f32[2048,3]{1,0:T(8,128)S(1)} %copy.389, f32[]{:T(128)} %constant.61.clone.1), kind=kCustom, calls=%fused_computation.64 | custom fusion | flops 6144 | bytes 18944 | tf_op jit(solution)/shard_map/scatter-add | solution.py:38
  167.1 6.4 %all-to-all-start.3 = ((f32[3,32,16]{2,0,1:T(4,128)}), f32[3,32,16]{2,0,1:T(4,128)}, u32[]{:S(2)}, u32[]{:S(2)}) async-start(f32[3,32,16]{2,0,1:T(4,128)} %copy.391), calls=%async_computation.3 | async-start | bytes 131072 | tf_op jit(solution)/shard_map/all_to_all | solution.py:143
  175.9 5.5 gather_fusion.8
  185.8 11.8 %scatter_custom_fusion.6 = f32[15,1536]{0,1:T(8,128)S(1)} fusion(s32[2048]{0:T(1024)} %bitcast.203, f32[2048,15]{1,0:T(8,128)S(1)} %copy.403, f32[]{:T(128)} %constant.61.clone.1), kind=kCustom, calls=%fused_computation.66 | custom fusion | flops 30720 | bytes 92672 | tf_op jit(solution)/shard_map/scatter-add | solution.py:38
  198.5 5.9 all-to-all-start.5
  206.2 11.7 %scatter_fusion.1 = f32[3,1024]{0,1:T(8,128)S(1)} fusion(f32[3,1024]{0,1:T(8,128)S(1)} %slice-done.3, s32[2048]{0:T(1024)S(1)} %bitcast.184, f32[2048,3]{1,0:T(8,128)S(1)} %copy.390), kind=kCustom, calls=%fused_computation.22 | custom fusion | flops 6144 | bytes 81920 | tf_op jit(solution)/shard_map/scatter-add | solution.py:38
  223.0 11.8 %scatter_fusion.2 = f32[15,1024]{0,1:T(8,128)S(1)} fusion(f32[15,1024]{0,1:T(8,128)S(1)} %slice-done, s32[2048]{0:T(1024)S(1)} %bitcast.185, f32[2048,15]{1,0:T(8,128)S(1)} %copy.404), kind=kCustom, calls=%fused_computation.25 | custom fusion | flops 30720 | bytes 376832 | tf_op jit(solution)/shard_map/scatter-add | solution.py:38
  240.8 40.7 %all-reduce.3 = (f32[]{:T(128)}, f32[1]{0:T(128)}) all-reduce(f32[]{:T(128)} %get-tuple-element.72, f32[1]{0:T(128)} %bitcast.41), channel_id=1, replica_groups=mesh['rows'=8,'sub'=4] {'rows','sub'}, use_global_device_ids=true, to_apply=%region_49.56 | all-reduce | flops 2 | bytes 16 | tf_op jit(solution)/shard_map/psum | solution.py:151
  285.9 5.5 gather_fusion.9
  292.4 4.7 all-to-all-start.6
  297.7 6.7 %all-to-all-done.6 = f32[3,32,16]{2,0,1:T(4,128)S(1)} async-done(((f32[3,32,16]{2,0,1:T(4,128)}), f32[3,32,16]{2,0,1:T(4,128)S(1)}, u32[]{:S(2)}, u32[]{:S(2)}) %all-to-all-start.6) | async-done | bytes 6176 | tf_op jit(solution)/shard_map/all_to_all | solution.py:139
  305.3 5.5 gather_fusion.11
  312.5 11.8 %scatter_custom_fusion.9 = f32[3,1536]{0,1:T(8,128)S(1)} fusion(s32[2048]{0:T(1024)} %bitcast.204, f32[2048,3]{1,0:T(8,128)S(1)} %copy.414, f32[]{:T(128)} %constant.61.clone.1), kind=kCustom, calls=%fused_computation.62 | custom fusion | flops 6144 | bytes 18944 | tf_op jit(solution)/shard_map/scatter-add | solution.py:38
  325.2 2.6 all-to-all-start.7
  328.9 11.9 %scatter_fusion.3 = f32[3,1024]{0,1:T(8,128)S(1)} fusion(f32[3,1024]{0,1:T(8,128)S(1)} %slice-done.4, s32[2048]{0:T(1024)S(1)} %bitcast.186, f32[2048,3]{1,0:T(8,128)S(1)} %copy.415), kind=kCustom, calls=%fused_computation.28 | custom fusion | flops 6144 | bytes 81920 | tf_op jit(solution)/shard_map/scatter-add | solution.py:38
  346.0 40.7 %all-reduce.2 = (f32[]{:T(128)}, f32[2]{0:T(128)S(1)}) all-reduce(f32[]{:T(128)} %get-tuple-element.69, f32[2]{0:T(128)S(1)} %pad_maximum_fusion.3), channel_id=1, replica_groups=mesh['rows'=8,'sub'=4] {'rows','sub'}, use_global_device_ids=true, to_apply=%region_62.69 | all-reduce | flops 3 | bytes 24 | tf_op jit(solution)/shard_map/psum | solution.py:151
  392.0 5.5 gather_fusion.12
  398.5 4.7 all-to-all-start.8
  403.9 6.7 %all-to-all-done.8 = f32[3,32,16]{2,0,1:T(4,128)S(1)} async-done(((f32[3,32,16]{2,0,1:T(4,128)}), f32[3,32,16]{2,0,1:T(4,128)S(1)}, u32[]{:S(2)}, u32[]{:S(2)}) %all-to-all-start.8) | async-done | bytes 6176 | tf_op jit(solution)/shard_map/all_to_all | solution.py:139
  411.0 5.5 gather_fusion.14
  417.9 11.8 %scatter_custom_fusion.12 = f32[3,1536]{0,1:T(8,128)S(1)} fusion(s32[2048]{0:T(1024)} %bitcast.205, f32[2048,3]{1,0:T(8,128)S(1)} %copy.428, f32[]{:T(128)} %constant.61.clone.1), kind=kCustom, calls=%fused_computation.60 | custom fusion | flops 6144 | bytes 18944 | tf_op jit(solution)/shard_map/scatter-add | solution.py:38
  430.6 2.6 all-to-all-start.9
  434.2 11.7 %scatter_fusion.4 = f32[3,1024]{0,1:T(8,128)S(1)} fusion(f32[3,1024]{0,1:T(8,128)S(1)} %slice-done.5, s32[2048]{0:T(1024)S(1)} %bitcast.187, f32[2048,3]{1,0:T(8,128)S(1)} %copy.429), kind=kCustom, calls=%fused_computation.31 | custom fusion | flops 6144 | bytes 81920 | tf_op jit(solution)/shard_map/scatter-add | solution.py:38
  446.4 2.8 scatter_custom_fusion.14
  452.0 40.7 %all-reduce.1 = (f32[]{:T(128)}, f32[3]{0:T(128)S(1)}) all-reduce(f32[]{:T(128)} %get-tuple-element.65, f32[3]{0:T(128)S(1)} %pad_maximum_fusion.4), channel_id=1, replica_groups=mesh['rows'=8,'sub'=4] {'rows','sub'}, use_global_device_ids=true, to_apply=%region_77.84 | all-reduce | flops 4 | bytes 32 | tf_op jit(solution)/shard_map/psum | solution.py:151
  498.4 5.5 gather_fusion.15
  504.9 4.6 all-to-all-start.10
  510.2 6.7 %all-to-all-done.10 = f32[3,32,16]{2,0,1:T(4,128)S(1)} async-done(((f32[3,32,16]{2,0,1:T(4,128)}), f32[3,32,16]{2,0,1:T(4,128)S(1)}, u32[]{:S(2)}, u32[]{:S(2)}) %all-to-all-start.10) | async-done | bytes 6176 | tf_op jit(solution)/shard_map/all_to_all | solution.py:139
  517.4 5.5 gather_fusion.17
  524.2 11.8 %scatter_custom_fusion.15 = f32[3,1536]{0,1:T(8,128)S(1)} fusion(s32[2048]{0:T(1024)} %bitcast.206, f32[2048,3]{1,0:T(8,128)S(1)} %copy.442, f32[]{:T(128)} %constant.61.clone.1), kind=kCustom, calls=%fused_computation.58 | custom fusion | flops 6144 | bytes 18944 | tf_op jit(solution)/shard_map/scatter-add | solution.py:38
  536.9 2.6 all-to-all-start.11
  540.6 11.7 %scatter_fusion.5 = f32[3,1024]{0,1:T(8,128)S(1)} fusion(f32[3,1024]{0,1:T(8,128)S(1)} %slice-done.2, s32[2048]{0:T(1024)S(1)} %bitcast.188, f32[2048,3]{1,0:T(8,128)S(1)} %copy.443), kind=kCustom, calls=%fused_computation.34 | custom fusion | flops 6144 | bytes 81920 | tf_op jit(solution)/shard_map/scatter-add | solution.py:38
  558.6 40.7 %all-reduce = (f32[]{:T(128)}, f32[4]{0:T(128)S(1)}) all-reduce(f32[]{:T(128)} %get-tuple-element.60, f32[4]{0:T(128)S(1)} %pad_maximum_fusion.5), channel_id=1, replica_groups=mesh['rows'=8,'sub'=4] {'rows','sub'}, use_global_device_ids=true, to_apply=%region_93.100 | all-reduce | flops 5 | bytes 40 | tf_op jit(solution)/shard_map/psum | solution.py:151
  604.5 3.0 subtract_divide_fusion
  (370 shorter events, 99.4 us)
Async XLA Ops:
  1.4 2.1 copy-start.49
  2.5 118.3 %copy-start.45 = (s32[1024]{0:T(1024)}, s32[1024]{0:T(1024)S(1)}, u32[]{:S(2)}) copy-start(s32[1024]{0:T(1024)S(1)} %pad_clamp_fusion) | copy-start | bytes 12292
  3.7 9.9 %copy-start.34 = (f32[36,2048]{1,0:T(8,128)S(1)}, f32[36,2048]{1,0:T(8,128)}, u32[]{:S(2)}) copy-start(f32[36,2048]{1,0:T(8,128)} %param.21) | copy-start | bytes 884740
  4.7 7.3 %copy-start.6 = (f32[15,1024]{1,0:T(8,128)S(1)}, f32[15,1024]{1,0:T(8,128)}, u32[]{:S(2)}) copy-start(f32[15,1024]{1,0:T(8,128)} %param.19) | copy-start | bytes 184324
  4.7 17.5 %all-to-all-start = ((f32[32,1,240]{2,1,0:T(1,128)}), f32[32,1,240]{2,1,0:T(1,128)S(1)}, u32[]{:S(2)}, u32[]{:S(2)}) async-start(f32[32,1,240]{2,1,0:T(1,128)} %reshape.1031), calls=%async_computation | async-start | bytes 65536 | tf_op jit(solution)/shard_map/all_to_all | solution.py:103
  12.8 101.0 %copy-start.30 = (s32[2048]{0:T(1024)}, s32[2048]{0:T(1024)S(1)}, u32[]{:S(2)}) copy-start(s32[2048]{0:T(1024)S(1)} %fusion.27) | copy-start | bytes 24580
  13.5 6.0 copy-start.41
  13.5 18.3 %copy-start.54 = (s32[2048,1]{0,1:T(1,128)}, s32[2048,1]{0,1:T(1,128)S(1)}, u32[]{:S(2)}) copy-start(s32[2048,1]{0,1:T(1,128)S(1)} %compare_select_fusion.1) | copy-start | bytes 24580
  13.5 10.7 %copy-start.22 = (s32[2048]{0:T(1024)}, s32[2048]{0:T(1024)S(1)}, u32[]{:S(2)}) copy-start(s32[2048]{0:T(1024)S(1)} %fusion.28) | copy-start | bytes 24580
  13.6 16.1 %copy-start.37 = (pred[2048]{0:T(1024)(128)(4,1)}, pred[2048]{0:T(1024)(128)(4,1)S(1)}, u32[]{:S(2)}) copy-start(pred[2048]{0:T(1024)(128)(4,1)S(1)} %compare_and_fusion) | copy-start | bytes 6148
  13.6 37.0 %copy-start.20 = (s32[2048,1]{0,1:T(1,128)}, s32[2048,1]{0,1:T(1,128)S(1)}, u32[]{:S(2)}) copy-start(s32[2048,1]{0,1:T(1,128)S(1)} %compare_select_fusion) | copy-start | bytes 24580
  13.6 50.4 %copy-start.55 = (s32[512,1]{0,1:T(1,128)}, s32[512,1]{0,1:T(1,128)S(1)}, u32[]{:S(2)}) copy-start(s32[512,1]{0,1:T(1,128)S(1)} %compare_select_fusion.4) | copy-start | bytes 6148
  14.0 7.6 %copy-start.11 = (f32[3,3,2048]{2,1,0:T(4,128)}, f32[3,3,2048]{2,1,0:T(4,128)S(1)}, u32[]{:S(2)}) copy-start(f32[3,3,2048]{2,1,0:T(4,128)S(1)} %get-tuple-element.99) | copy-start | bytes 221188
  14.0 7.6 %copy-start.13 = (f32[3,3,2048]{2,1,0:T(4,128)}, f32[3,3,2048]{2,1,0:T(4,128)S(1)}, u32[]{:S(2)}) copy-start(f32[3,3,2048]{2,1,0:T(4,128)S(1)} %get-tuple-element.100) | copy-start | bytes 221188
  14.0 16.4 %copy-start.7 = (f32[3,3,2048]{2,1,0:T(4,128)}, f32[3,3,2048]{2,1,0:T(4,128)S(1)}, u32[]{:S(2)}) copy-start(f32[3,3,2048]{2,1,0:T(4,128)S(1)} %get-tuple-element.97) | copy-start | bytes 221188
  14.0 16.4 %copy-start.9 = (f32[3,3,2048]{2,1,0:T(4,128)}, f32[3,3,2048]{2,1,0:T(4,128)S(1)}, u32[]{:S(2)}) copy-start(f32[3,3,2048]{2,1,0:T(4,128)S(1)} %get-tuple-element.98) | copy-start | bytes 221188
  22.3 9.1 %copy-start.26 = (f32[2048]{0:T(1024)}, f32[2048]{0:T(1024)S(1)}, u32[]{:S(2)}) copy-start(f32[2048]{0:T(1024)S(1)} %fusion.26) | copy-start | bytes 24580
  43.4 6.7 %copy-start.1 = (f32[15,1536]{0,1:T(8,128)}, f32[15,1536]{0,1:T(8,128)S(1)}, u32[]{:S(2)}) copy-start(f32[15,1536]{0,1:T(8,128)S(1)} %scatter_custom_fusion) | copy-start | bytes 276484
  44.3 18.8 %all-to-all-start.1 = ((f32[32,1,240]{2,1,0:T(1,128)}), f32[32,1,240]{2,1,0:T(1,128)S(1)}, u32[]{:S(2)}, u32[]{:S(2)}) async-start(f32[32,1,240]{2,1,0:T(1,128)} %reshape.1033), calls=%async_computation.1 | async-start | bytes 65536 | tf_op jit(solution)/shard_map/all_to_all | solution.py:107
  120.8 1.7 copy-start.31
  127.9 1.1 copy-start.35
  127.9 1.1 copy-start.50
  130.0 12.3 %all-to-all-start.2 = ((f32[3,32,16]{2,0,1:T(4,128)}), f32[3,32,16]{2,0,1:T(4,128)}, u32[]{:S(2)}, u32[]{:S(2)}) async-start(f32[3,32,16]{2,0,1:T(4,128)} %copy.385), calls=%async_computation.2 | async-start | bytes 131072 | tf_op jit(solution)/shard_map/all_to_all | solution.py:139
  134.9 1.1 copy-start.33
  134.9 1.1 copy-start.51
  142.2 24.8 %all-to-all-start.4 = ((f32[32,1,240]{2,1,0:T(1,128)}), f32[32,1,240]{2,1,0:T(1,128)S(1)}, u32[]{:S(2)}, u32[]{:S(2)}) async-start(f32[32,1,240]{2,1,0:T(1,128)} %reshape.1035), calls=%async_computation.4 | async-start | bytes 65536 | tf_op jit(solution)/shard_map/all_to_all | solution.py:120
  146.5 5.5 copy-start.38
  166.1 38.3 %copy-start.3 = (f32[3,1536]{0,1:T(8,128)}, f32[3,1536]{0,1:T(8,128)S(1)}, u32[]{:S(2)}) copy-start(f32[3,1536]{0,1:T(8,128)S(1)} %scatter_custom_fusion.3) | copy-start | bytes 55300
  167.1 31.4 %all-to-all-start.3 = ((f32[3,32,16]{2,0,1:T(4,128)}), f32[3,32,16]{2,0,1:T(4,128)}, u32[]{:S(2)}, u32[]{:S(2)}) async-start(f32[3,32,16]{2,0,1:T(4,128)} %copy.391), calls=%async_computation.3 | async-start | bytes 131072 | tf_op jit(solution)/shard_map/all_to_all | solution.py:143
  175.9 5.5 copy-start.39
  197.5 24.4 %copy-start = (f32[15,1536]{0,1:T(8,128)}, f32[15,1536]{0,1:T(8,128)S(1)}, u32[]{:S(2)}) copy-start(f32[15,1536]{0,1:T(8,128)S(1)} %scatter_custom_fusion.6) | copy-start | bytes 276484
  198.5 36.4 %all-to-all-start.5 = ((f32[32,1,240]{2,1,0:T(1,128)}), f32[32,1,240]{2,1,0:T(1,128)S(1)}, u32[]{:S(2)}, u32[]{:S(2)}) async-start(f32[32,1,240]{2,1,0:T(1,128)} %reshape.1037), calls=%async_computation.5 | async-start | bytes 65536 | tf_op jit(solution)/shard_map/all_to_all | solution.py:124
  221.9 1.1 slice-start
  285.8 5.5 copy-start.52
  292.4 4.7 copy-start.42
  292.4 12.1 %all-to-all-start.6 = ((f32[3,32,16]{2,0,1:T(4,128)}), f32[3,32,16]{2,0,1:T(4,128)S(1)}, u32[]{:S(2)}, u32[]{:S(2)}) async-start(f32[3,32,16]{2,0,1:T(4,128)} %copy.410), calls=%async_computation.6 | async-start | bytes 131072 | tf_op jit(solution)/shard_map/all_to_all | solution.py:139
  305.3 5.5 copy-start.40
  324.3 3.5 copy-start.4
  325.2 15.8 %all-to-all-start.7 = ((f32[3,32,16]{2,0,1:T(4,128)}), f32[3,32,16]{2,0,1:T(4,128)S(1)}, u32[]{:S(2)}, u32[]{:S(2)}) async-start(f32[3,32,16]{2,0,1:T(4,128)} %copy.416), calls=%async_computation.7 | async-start | bytes 131072 | tf_op jit(solution)/shard_map/all_to_all | solution.py:143
  327.8 1.0 slice-start.4
  398.5 12.1 %all-to-all-start.8 = ((f32[3,32,16]{2,0,1:T(4,128)}), f32[3,32,16]{2,0,1:T(4,128)S(1)}, u32[]{:S(2)}, u32[]{:S(2)}) async-start(f32[3,32,16]{2,0,1:T(4,128)} %copy.424), calls=%async_computation.8 | async-start | bytes 131072 | tf_op jit(solution)/shard_map/all_to_all | solution.py:139
  429.7 3.5 copy-start.5
  430.6 15.5 %all-to-all-start.9 = ((f32[3,32,16]{2,0,1:T(4,128)}), f32[3,32,16]{2,0,1:T(4,128)S(1)}, u32[]{:S(2)}, u32[]{:S(2)}) async-start(f32[3,32,16]{2,0,1:T(4,128)} %copy.430), calls=%async_computation.9 | async-start | bytes 131072 | tf_op jit(solution)/shard_map/all_to_all | solution.py:143
  433.2 1.0 slice-start.5
  504.9 12.0 %all-to-all-start.10 = ((f32[3,32,16]{2,0,1:T(4,128)}), f32[3,32,16]{2,0,1:T(4,128)S(1)}, u32[]{:S(2)}, u32[]{:S(2)}) async-start(f32[3,32,16]{2,0,1:T(4,128)} %copy.438), calls=%async_computation.10 | async-start | bytes 131072 | tf_op jit(solution)/shard_map/all_to_all | solution.py:139
  536.0 3.5 copy-start.2
  536.9 15.5 %all-to-all-start.11 = ((f32[3,32,16]{2,0,1:T(4,128)}), f32[3,32,16]{2,0,1:T(4,128)S(1)}, u32[]{:S(2)}, u32[]{:S(2)}) async-start(f32[3,32,16]{2,0,1:T(4,128)} %copy.444), calls=%async_computation.11 | async-start | bytes 131072 | tf_op jit(solution)/shard_map/all_to_all | solution.py:143
  539.5 1.0 slice-start.2
  (26 other events, 21.2 us)
where the time goes:
time: 619 us; the launch traced here: 608 us
  blocking collectives  204 us (33%)
  other arithmetic  195 us (32%)
  local copies, waits for them, and re-layouts  120 us (19%)
  starting transfers between devices  54.6 us (9%)
  waiting for transfers between devices  24 us (4%)
  between operations  11.7 us (2%)
    psum x4, blocking collectives, on_device(): lax.psum((local_dots, jnp.sum(image_vec * image_vec)), ('rows', 'sub'))  163 us
    scatter-add x18, other arithmetic, add_columns(): return total.at[:, index].add(values, mode='drop')  156 us
    gather x18, local copies, waits for them, and re-layouts, take_columns(): return jnp.take(table, index, axis=1, mode='fill', fill_value=0.0)  73 us
    psum x1, blocking collectives, on_device(): total_square = lax.psum(jnp.sum(gradient * gradient), ('rows', 'sub'))  40.7 us
    all_to_all x4, waiting for transfers between devices, on_device(): lax.all_to_all(pack_rows(vector, send_row), ('rows', 'sub'), split_axis=1...  23.9 us
    all_to_all x4, starting transfers between devices, on_device(): lax.all_to_all(pack_rows(vector, send_row), ('rows', 'sub'), split_axis=1...  18.9 us
    unnamed x121, local copies, waits for them, and re-layouts  14.4 us
    all_to_all x4, starting transfers between devices, on_device(): lax.all_to_all(far_vector.reshape(DIM, -1), ('rows', 'sub'), split_axis=1...  14.1 us
  transfers between devices with their start and end apart: 12, of which 4 were waited for; matrix products, arithmetic and copies ran while one was open for 22% of the time, Pallas kernels for 0%

commit v1 on v0

--- a/solution.py
+++ b/solution.py
@@ -136,8 +136,16 @@
     beta_list = []
     for iteration in range(LANCZOS):
         vector = krylov_basis[-1]
-        halo_vector = lax.all_to_all(
-            pack_rows(vector, send_row), ("rows", "sub"), split_axis=1, concat_axis=1, tiled=True
+        halo_vector = jnp.concatenate(
+            lax.all_to_all(
+                jnp.stack(
+                    jnp.split(pack_rows(vector, send_row), lax.axis_size(("rows", "sub")), axis=1)
+                ),
+                ("rows", "sub"),
+                0,
+                0,
+            ),
+            axis=1,
         )
         near_vector, far_vector = split_product(vector, halo_vector)
         returned_vector = lax.all_to_all(

time: 619 us -> 713 us (1.15)
  local copies, waits for them, and re-layouts: 120 us -> 212 us
    unnamed x121 -> x303, local copies, waits for them, and re-layouts: 14.4 us -> 96.6 us
    split x0 -> x136, local copies, waits for them, and re-layouts: none -> 12.3 us  [on_device(): jnp.split(pack_rows(vector, send_row), lax.axis_size(('rows', 'sub')), ax...]
  transfers between devices with their start and end apart: 12 -> 12, of which waited for: 4 -> 4; matrix products, arithmetic and copies ran while one was open for 22% -> 19% of each run, Pallas kernels for 0% -> 0%
where the time goes in v1:
time: 713 us; the launch traced here: 701 us
  local copies, waits for them, and re-layouts  212 us (30%)
  blocking collectives  203 us (28%)
  other arithmetic  195 us (27%)
  starting transfers between devices  54.6 us (8%)
  waiting for transfers between devices  23.9 us (3%)
  between operations  11.9 us (2%)
    psum x4, blocking collectives, on_device(): lax.psum((local_dots, jnp.sum(image_vec * image_vec)), ('rows', 'sub'))  163 us
    scatter-add x18, other arithmetic, add_columns(): return total.at[:, index].add(values, mode='drop')  157 us
    unnamed x303, local copies, waits for them, and re-layouts  96.6 us
    gather x18, local copies, waits for them, and re-layouts, take_columns(): return jnp.take(table, index, axis=1, mode='fill', fill_value=0.0)  72.4 us
    psum x1, blocking collectives, on_device(): total_square = lax.psum(jnp.sum(gradient * gradient), ('rows', 'sub'))  40.7 us
    all_to_all x4, waiting for transfers between devices, on_device(): lax.all_to_all(jnp.stack(jnp.split(pack_rows(vector, send_row), lax.axis_...  23.9 us
    all_to_all x4, starting transfers between devices, on_device(): lax.all_to_all(jnp.stack(jnp.split(pack_rows(vector, send_row), lax.axis_...  18.9 us
  transfers between devices with their start and end apart: 12, of which 4 were waited for; matrix products, arithmetic and copies ran while one was open for 19% of the time, Pallas kernels for 0%

profile of v1, /device:TPU:0, one launch (start us, length us, event | category | flops | bytes accessed | tf_op | source)
XLA Modules:
  0.0 701.1 jit_solution(383724269607353366)
XLA Ops:
  4.7 7.3 %all-to-all-start = ((f32[32,1,240]{2,1,0:T(1,128)}), f32[32,1,240]{2,1,0:T(1,128)S(1)}, u32[]{:S(2)}, u32[]{:S(2)}) async-start(f32[32,1,240]{2,1,0:T(1,128)} %reshape.1019), calls=%async_computation | async-start | bytes 65536 | tf_op jit(solution)/shard_map/all_to_all | solution.py:103
  14.0 5.5 gather_fusion
  24.2 5.5 gather_fusion.2
  31.8 11.7 %scatter_custom_fusion = f32[15,1536]{0,1:T(8,128)S(1)} fusion(s32[2048]{0:T(1024)S(1)} %bitcast.456, f32[2048,15]{1,0:T(8,128)S(1)} %copy.1525, f32[]{:T(128)} %constant.61.clone.1), kind=kCustom, calls=%fused_computation.68 | custom fusion | flops 30720 | bytes 92164 | tf_op jit(solution)/shard_map/scatter-add | solution.py:38
  44.3 5.8 all-to-all-start.1
  51.2 11.7 %scatter_fusion = f32[15,1024]{0,1:T(8,128)S(1)} fusion(f32[15,1024]{0,1:T(8,128)S(1)} %slice-done.1, s32[2048]{0:T(1024)S(1)} %bitcast.435, f32[2048,15]{1,0:T(8,128)S(1)} %copy.1526), kind=kCustom, calls=%fused_computation.19 | custom fusion | flops 30720 | bytes 376832 | tf_op jit(solution)/shard_map/scatter-add | solution.py:38
  64.0 2.6 scatter_custom_fusion.2
  67.7 40.7 %all-reduce.4 = (f32[]{:T(128)}, f32[]{:T(128)}) all-reduce(f32[]{:T(128)} %get-tuple-element.95, f32[]{:T(128)} %multiply_reduce_fusion.63), channel_id=1, replica_groups=mesh['rows'=8,'sub'=4] {'rows','sub'}, use_global_device_ids=true, to_apply=%region_10.14 | all-reduce | flops 2 | bytes 16 | tf_op jit(solution)/shard_map/psum | solution.py:115
  113.7 5.5 gather_fusion.6
  123.3 5.5 gather_fusion.3
  161.0 4.9 all-to-all-start.2
  169.5 3.7 all-to-all-done.2
  173.3 2.6 all-to-all-start.4
  177.5 5.5 gather_fusion.5
  185.3 11.8 %scatter_custom_fusion.3 = f32[3,1536]{0,1:T(8,128)S(1)} fusion(s32[2048]{0:T(1024)} %bitcast.457, f32[2048,3]{1,0:T(8,128)S(1)} %copy.1568, f32[]{:T(128)} %constant.61.clone.1), kind=kCustom, calls=%fused_computation.64 | custom fusion | flops 6144 | bytes 18944 | tf_op jit(solution)/shard_map/scatter-add | solution.py:38
  198.1 6.4 all-to-all-start.3
  206.9 5.5 gather_fusion.8
  216.8 11.8 %scatter_custom_fusion.6 = f32[15,1536]{0,1:T(8,128)S(1)} fusion(s32[2048]{0:T(1024)} %bitcast.458, f32[2048,15]{1,0:T(8,128)S(1)} %copy.1582, f32[]{:T(128)} %constant.61.clone.1), kind=kCustom, calls=%fused_computation.66 | custom fusion | flops 30720 | bytes 92672 | tf_op jit(solution)/shard_map/scatter-add | solution.py:38
  229.5 5.9 all-to-all-start.5
  237.2 11.7 %scatter_fusion.1 = f32[3,1024]{0,1:T(8,128)S(1)} fusion(f32[3,1024]{0,1:T(8,128)S(1)} %slice-done.3, s32[2048]{0:T(1024)S(1)} %bitcast.436, f32[2048,3]{1,0:T(8,128)S(1)} %copy.1569), kind=kCustom, calls=%fused_computation.22 | custom fusion | flops 6144 | bytes 81920 | tf_op jit(solution)/shard_map/scatter-add | solution.py:38
  250.2 2.5 scatter_custom_fusion.5
  254.0 11.8 %scatter_fusion.2 = f32[15,1024]{0,1:T(8,128)S(1)} fusion(f32[15,1024]{0,1:T(8,128)S(1)} %slice-done, s32[2048]{0:T(1024)S(1)} %bitcast.437, f32[2048,15]{1,0:T(8,128)S(1)} %copy.1583), kind=kCustom, calls=%fused_computation.25 | custom fusion | flops 30720 | bytes 376832 | tf_op jit(solution)/shard_map/scatter-add | solution.py:38
  271.8 40.7 %all-reduce.3 = (f32[]{:T(128)}, f32[1]{0:T(128)}) all-reduce(f32[]{:T(128)} %get-tuple-element.72, f32[1]{0:T(128)} %bitcast.73), channel_id=1, replica_groups=mesh['rows'=8,'sub'=4] {'rows','sub'}, use_global_device_ids=true, to_apply=%region_49.56 | all-reduce | flops 2 | bytes 16 | tf_op jit(solution)/shard_map/psum | solution.py:159
  317.7 5.5 gather_fusion.9
  344.4 4.7 all-to-all-start.6
  349.7 6.7 all-to-all-done.6
  357.3 5.5 gather_fusion.11
  364.5 11.8 %scatter_custom_fusion.9 = f32[3,1536]{0,1:T(8,128)S(1)} fusion(s32[2048]{0:T(1024)} %bitcast.459, f32[2048,3]{1,0:T(8,128)S(1)} %copy.1624, f32[]{:T(128)} %constant.61.clone.1), kind=kCustom, calls=%fused_computation.62 | custom fusion | flops 6144 | bytes 18944 | tf_op jit(solution)/shard_map/scatter-add | solution.py:38
  377.2 2.6 all-to-all-start.7
  380.9 11.9 %scatter_fusion.3 = f32[3,1024]{0,1:T(8,128)S(1)} fusion(f32[3,1024]{0,1:T(8,128)S(1)} %slice-done.4, s32[2048]{0:T(1024)S(1)} %bitcast.438, f32[2048,3]{1,0:T(8,128)S(1)} %copy.1625), kind=kCustom, calls=%fused_computation.28 | custom fusion | flops 6144 | bytes 81920 | tf_op jit(solution)/shard_map/scatter-add | solution.py:38
  398.0 40.7 %all-reduce.2 = (f32[]{:T(128)}, f32[2]{0:T(128)S(1)}) all-reduce(f32[]{:T(128)} %get-tuple-element.69, f32[2]{0:T(128)S(1)} %pad_maximum_fusion.3), channel_id=1, replica_groups=mesh['rows'=8,'sub'=4] {'rows','sub'}, use_global_device_ids=true, to_apply=%region_62.69 | all-reduce | flops 3 | bytes 24 | tf_op jit(solution)/shard_map/psum | solution.py:159
  444.2 5.5 gather_fusion.12
  470.9 4.7 all-to-all-start.8
  476.3 6.7 all-to-all-done.8
  483.4 5.5 gather_fusion.14
  490.3 11.8 %scatter_custom_fusion.12 = f32[3,1536]{0,1:T(8,128)S(1)} fusion(s32[2048]{0:T(1024)} %bitcast.460, f32[2048,3]{1,0:T(8,128)S(1)} %copy.1669, f32[]{:T(128)} %constant.61.clone.1), kind=kCustom, calls=%fused_computation.60 | custom fusion | flops 6144 | bytes 18944 | tf_op jit(solution)/shard_map/scatter-add | solution.py:38
  503.0 2.6 all-to-all-start.9
  506.6 11.9 %scatter_fusion.4 = f32[3,1024]{0,1:T(8,128)S(1)} fusion(f32[3,1024]{0,1:T(8,128)S(1)} %slice-done.5, s32[2048]{0:T(1024)S(1)} %bitcast.439, f32[2048,3]{1,0:T(8,128)S(1)} %copy.1670), kind=kCustom, calls=%fused_computation.31 | custom fusion | flops 6144 | bytes 81920 | tf_op jit(solution)/shard_map/scatter-add | solution.py:38
  524.4 40.7 %all-reduce.1 = (f32[]{:T(128)}, f32[3]{0:T(128)S(1)}) all-reduce(f32[]{:T(128)} %get-tuple-element.65, f32[3]{0:T(128)S(1)} %pad_maximum_fusion.4), channel_id=1, replica_groups=mesh['rows'=8,'sub'=4] {'rows','sub'}, use_global_device_ids=true, to_apply=%region_77.84 | all-reduce | flops 4 | bytes 32 | tf_op jit(solution)/shard_map/psum | solution.py:159
  571.0 5.5 gather_fusion.15
  597.7 4.6 all-to-all-start.10
  603.0 6.7 all-to-all-done.10
  610.1 5.5 gather_fusion.17
  617.0 11.8 %scatter_custom_fusion.15 = f32[3,1536]{0,1:T(8,128)S(1)} fusion(s32[2048]{0:T(1024)} %bitcast.461, f32[2048,3]{1,0:T(8,128)S(1)} %copy.1714, f32[]{:T(128)} %constant.61.clone.1), kind=kCustom, calls=%fused_computation.58 | custom fusion | flops 6144 | bytes 18944 | tf_op jit(solution)/shard_map/scatter-add | solution.py:38
  629.7 2.6 all-to-all-start.11
  633.3 12.0 %scatter_fusion.5 = f32[3,1024]{0,1:T(8,128)S(1)} fusion(f32[3,1024]{0,1:T(8,128)S(1)} %slice-done.2, s32[2048]{0:T(1024)S(1)} %bitcast.440, f32[2048,3]{1,0:T(8,128)S(1)} %copy.1715), kind=kCustom, calls=%fused_computation.34 | custom fusion | flops 6144 | bytes 81920 | tf_op jit(solution)/shard_map/scatter-add | solution.py:38
  651.7 40.7 %all-reduce = (f32[]{:T(128)}, f32[4]{0:T(128)S(1)}) all-reduce(f32[]{:T(128)} %get-tuple-element.60, f32[4]{0:T(128)S(1)} %pad_maximum_fusion.5), channel_id=1, replica_groups=mesh['rows'=8,'sub'=4] {'rows','sub'}, use_global_device_ids=true, to_apply=%region_93.100 | all-reduce | flops 5 | bytes 40 | tf_op jit(solution)/shard_map/psum | solution.py:159
  697.5 3.0 subtract_divide_fusion
  (688 shorter events, 192.0 us)
Async XLA Ops:
  1.4 120.4 %copy-start.79 = (pred[512]{0:T(512)(128)(4,1)}, pred[512]{0:T(512)(128)(4,1)S(1)}, u32[]{:S(2)}) copy-start(pred[512]{0:T(512)(128)(4,1)S(1)} %compare_and_fusion.2) | copy-start | bytes 1540
  2.5 118.2 %copy-start.44 = (s32[1024]{0:T(1024)}, s32[1024]{0:T(1024)S(1)}, u32[]{:S(2)}) copy-start(s32[1024]{0:T(1024)S(1)} %pad_clamp_fusion) | copy-start | bytes 12292
  3.7 9.9 %copy-start.34 = (f32[36,2048]{1,0:T(8,128)S(1)}, f32[36,2048]{1,0:T(8,128)}, u32[]{:S(2)}) copy-start(f32[36,2048]{1,0:T(8,128)} %param.21) | copy-start | bytes 884740
  4.7 7.3 %copy-start.6 = (f32[15,1024]{1,0:T(8,128)S(1)}, f32[15,1024]{1,0:T(8,128)}, u32[]{:S(2)}) copy-start(f32[15,1024]{1,0:T(8,128)} %param.19) | copy-start | bytes 184324
  4.7 17.5 %all-to-all-start = ((f32[32,1,240]{2,1,0:T(1,128)}), f32[32,1,240]{2,1,0:T(1,128)S(1)}, u32[]{:S(2)}, u32[]{:S(2)}) async-start(f32[32,1,240]{2,1,0:T(1,128)} %reshape.1019), calls=%async_computation | async-start | bytes 65536 | tf_op jit(solution)/shard_map/all_to_all | solution.py:103
  12.8 101.0 %copy-start.30 = (s32[2048]{0:T(1024)}, s32[2048]{0:T(1024)S(1)}, u32[]{:S(2)}) copy-start(s32[2048]{0:T(1024)S(1)} %fusion.27) | copy-start | bytes 24580
  13.5 6.0 copy-start.40
  13.5 18.3 %copy-start.83 = (s32[2048,1]{0,1:T(1,128)}, s32[2048,1]{0,1:T(1,128)S(1)}, u32[]{:S(2)}) copy-start(s32[2048,1]{0,1:T(1,128)S(1)} %compare_select_fusion.1) | copy-start | bytes 24580
  13.5 10.7 %copy-start.22 = (s32[2048]{0:T(1024)}, s32[2048]{0:T(1024)S(1)}, u32[]{:S(2)}) copy-start(s32[2048]{0:T(1024)S(1)} %fusion.28) | copy-start | bytes 24580
  13.6 16.1 %copy-start.36 = (pred[2048]{0:T(1024)(128)(4,1)}, pred[2048]{0:T(1024)(128)(4,1)S(1)}, u32[]{:S(2)}) copy-start(pred[2048]{0:T(1024)(128)(4,1)S(1)} %compare_and_fusion) | copy-start | bytes 6148
  13.6 37.0 %copy-start.20 = (s32[2048,1]{0,1:T(1,128)}, s32[2048,1]{0,1:T(1,128)S(1)}, u32[]{:S(2)}) copy-start(s32[2048,1]{0,1:T(1,128)S(1)} %compare_select_fusion) | copy-start | bytes 24580
  13.6 50.4 %copy-start.84 = (s32[512,1]{0,1:T(1,128)}, s32[512,1]{0,1:T(1,128)S(1)}, u32[]{:S(2)}) copy-start(s32[512,1]{0,1:T(1,128)S(1)} %compare_select_fusion.4) | copy-start | bytes 6148
  14.0 7.6 %copy-start.11 = (f32[3,3,2048]{2,1,0:T(4,128)}, f32[3,3,2048]{2,1,0:T(4,128)S(1)}, u32[]{:S(2)}) copy-start(f32[3,3,2048]{2,1,0:T(4,128)S(1)} %get-tuple-element.99) | copy-start | bytes 221188
  14.0 7.6 %copy-start.13 = (f32[3,3,2048]{2,1,0:T(4,128)}, f32[3,3,2048]{2,1,0:T(4,128)S(1)}, u32[]{:S(2)}) copy-start(f32[3,3,2048]{2,1,0:T(4,128)S(1)} %get-tuple-element.100) | copy-start | bytes 221188
  14.0 16.4 %copy-start.7 = (f32[3,3,2048]{2,1,0:T(4,128)}, f32[3,3,2048]{2,1,0:T(4,128)S(1)}, u32[]{:S(2)}) copy-start(f32[3,3,2048]{2,1,0:T(4,128)S(1)} %get-tuple-element.97) | copy-start | bytes 221188
  14.0 16.4 %copy-start.9 = (f32[3,3,2048]{2,1,0:T(4,128)}, f32[3,3,2048]{2,1,0:T(4,128)S(1)}, u32[]{:S(2)}) copy-start(f32[3,3,2048]{2,1,0:T(4,128)S(1)} %get-tuple-element.98) | copy-start | bytes 221188
  22.2 9.1 %copy-start.26 = (f32[2048]{0:T(1024)}, f32[2048]{0:T(1024)S(1)}, u32[]{:S(2)}) copy-start(f32[2048]{0:T(1024)S(1)} %fusion.26) | copy-start | bytes 24580
  43.4 6.7 copy-start.1
  44.3 18.8 %all-to-all-start.1 = ((f32[32,1,240]{2,1,0:T(1,128)}), f32[32,1,240]{2,1,0:T(1,128)S(1)}, u32[]{:S(2)}, u32[]{:S(2)}) async-start(f32[32,1,240]{2,1,0:T(1,128)} %reshape.1021), calls=%async_computation.1 | async-start | bytes 65536 | tf_op jit(solution)/shard_map/all_to_all | solution.py:107
  50.2 1.0 slice-start.1
  129.8 1.4 copy-start.78
  161.0 12.3 %all-to-all-start.2 = ((f32[32,3,16]{2,1,0:T(4,128)}), f32[32,3,16]{2,1,0:T(4,128)}, u32[]{:S(2)}, u32[]{:S(2)}) async-start(f32[32,3,16]{2,1,0:T(4,128)} %constant_dynamic-update-slice_fusion), calls=%async_computation.2 | async-start | bytes 131072 | tf_op jit(solution)/shard_map/all_to_all | solution.py:140
  165.9 1.1 copy-start.33
  165.9 1.1 copy-start.80
  173.3 24.8 %all-to-all-start.4 = ((f32[32,1,240]{2,1,0:T(1,128)}), f32[32,1,240]{2,1,0:T(1,128)S(1)}, u32[]{:S(2)}, u32[]{:S(2)}) async-start(f32[32,1,240]{2,1,0:T(1,128)} %reshape.1023), calls=%async_computation.4 | async-start | bytes 65536 | tf_op jit(solution)/shard_map/all_to_all | solution.py:120
  177.5 5.5 copy-start.37
  197.1 38.3 %copy-start.3 = (f32[3,1536]{0,1:T(8,128)}, f32[3,1536]{0,1:T(8,128)S(1)}, u32[]{:S(2)}) copy-start(f32[3,1536]{0,1:T(8,128)S(1)} %scatter_custom_fusion.3) | copy-start | bytes 55300
  198.1 31.4 %all-to-all-start.3 = ((f32[3,32,16]{2,0,1:T(4,128)}), f32[3,32,16]{2,0,1:T(4,128)}, u32[]{:S(2)}, u32[]{:S(2)}) async-start(f32[3,32,16]{2,0,1:T(4,128)} %copy.1570), calls=%async_computation.3 | async-start | bytes 131072 | tf_op jit(solution)/shard_map/all_to_all | solution.py:151
  206.9 5.5 copy-start.38
  228.5 24.4 %copy-start = (f32[15,1536]{0,1:T(8,128)}, f32[15,1536]{0,1:T(8,128)S(1)}, u32[]{:S(2)}) copy-start(f32[15,1536]{0,1:T(8,128)S(1)} %scatter_custom_fusion.6) | copy-start | bytes 276484
  229.5 36.4 %all-to-all-start.5 = ((f32[32,1,240]{2,1,0:T(1,128)}), f32[32,1,240]{2,1,0:T(1,128)S(1)}, u32[]{:S(2)}, u32[]{:S(2)}) async-start(f32[32,1,240]{2,1,0:T(1,128)} %reshape.1025), calls=%async_computation.5 | async-start | bytes 65536 | tf_op jit(solution)/shard_map/all_to_all | solution.py:124
  236.2 1.0 slice-start.3
  236.2 1.0 copy-start.21
  252.9 1.1 slice-start
  344.4 4.7 copy-start.41
  344.4 12.1 %all-to-all-start.6 = ((f32[32,3,16]{2,1,0:T(4,128)}), f32[32,3,16]{2,1,0:T(4,128)S(1)}, u32[]{:S(2)}, u32[]{:S(2)}) async-start(f32[32,3,16]{2,1,0:T(4,128)} %constant_dynamic-update-slice_fusion.32), calls=%async_computation.6 | async-start | bytes 131072 | tf_op jit(solution)/shard_map/all_to_all | solution.py:140
  357.3 5.5 copy-start.39
  376.3 3.5 copy-start.4
  377.2 15.8 %all-to-all-start.7 = ((f32[3,32,16]{2,0,1:T(4,128)}), f32[3,32,16]{2,0,1:T(4,128)S(1)}, u32[]{:S(2)}, u32[]{:S(2)}) async-start(f32[3,32,16]{2,0,1:T(4,128)} %copy.1626), calls=%async_computation.7 | async-start | bytes 131072 | tf_op jit(solution)/shard_map/all_to_all | solution.py:151
  379.9 1.0 slice-start.4
  470.9 12.1 %all-to-all-start.8 = ((f32[32,3,16]{2,1,0:T(4,128)}), f32[32,3,16]{2,1,0:T(4,128)S(1)}, u32[]{:S(2)}, u32[]{:S(2)}) async-start(f32[32,3,16]{2,1,0:T(4,128)} %constant_dynamic-update-slice_fusion.64), calls=%async_computation.8 | async-start | bytes 131072 | tf_op jit(solution)/shard_map/all_to_all | solution.py:140
  502.0 3.5 copy-start.5
  503.0 15.8 %all-to-all-start.9 = ((f32[3,32,16]{2,0,1:T(4,128)}), f32[3,32,16]{2,0,1:T(4,128)S(1)}, u32[]{:S(2)}, u32[]{:S(2)}) async-start(f32[3,32,16]{2,0,1:T(4,128)} %copy.1671), calls=%async_computation.9 | async-start | bytes 131072 | tf_op jit(solution)/shard_map/all_to_all | solution.py:151
  505.6 1.0 slice-start.5
  597.7 12.0 %all-to-all-start.10 = ((f32[32,3,16]{2,1,0:T(4,128)}), f32[32,3,16]{2,1,0:T(4,128)S(1)}, u32[]{:S(2)}, u32[]{:S(2)}) async-start(f32[32,3,16]{2,1,0:T(4,128)} %constant_dynamic-update-slice_fusion.96), calls=%async_computation.10 | async-start | bytes 131072 | tf_op jit(solution)/shard_map/all_to_all | solution.py:140
  628.8 3.5 copy-start.2
  629.7 15.8 %all-to-all-start.11 = ((f32[3,32,16]{2,0,1:T(4,128)}), f32[3,32,16]{2,0,1:T(4,128)S(1)}, u32[]{:S(2)}, u32[]{:S(2)}) async-start(f32[3,32,16]{2,0,1:T(4,128)} %copy.1716), calls=%async_computation.11 | async-start | bytes 131072 | tf_op jit(solution)/shard_map/all_to_all | solution.py:151
  632.3 1.0 slice-start.2
  (55 other events, 40.5 us)
